TPU v7x, 32 devices: a whole 2x2x4 slice. The times are simulated.
32 devices in a mesh: row: 8 (over y, x, core), col: 4 (over z).
Axes of the slice: x: 2, y: 2, z: 4, core: 2. Of those that a mesh axis runs over, the one named last changes fastest.
Arguments:
- coeffs: float32 [2, 12288, 2048], P(None, ('row', 'col')), may hold values from -6 to 6
- forces: float32 [2, 12288, 2048], P(None, ('row', 'col')), may hold values from -6 to 6
- multipliers: float32 [2048, 2048], P('row', 'col'), may hold values from -0.125 to 0.125
Outputs:
- constrained: float32 [2, 12288, 2048], P(None, ('row', 'col'))
All inputs are finite; a program needn't handle non-finite values.
Results may differ from a plain program's by a relative error of at most 0.000051.
Values sent between devices are 32-bit elements; how exact they have to be, the bound alone decides.
A program may use at most 128 MiB of HBM per device.

v0:
```python
import jax
import jax.numpy as jnp
from jax import lax
from jax.sharding import PartitionSpec as P


def body(coeffs, forces, multipliers):
    stacked = coeffs.reshape(2 * coeffs.shape[1], coeffs.shape[2])
    panel = lax.all_gather(multipliers, "col", axis=1, tiled=True)
    product = jnp.dot(
        stacked,
        lax.all_gather(panel, "row", axis=0, tiled=True),
        precision=lax.Precision.HIGHEST,
        preferred_element_type=jnp.float32,
    )
    return forces - product.reshape(coeffs.shape)


def solution(mesh):
    placed = (P(None, ("row", "col"), None), P(None, ("row", "col"), None), P("row", "col"))
    return jax.shard_map(
        body, mesh=mesh, in_specs=placed, out_specs=P(None, ("row", "col"), None), check_vma=False
    )
```

profile of v0, /device:TPU:0, one launch (start us, length us, event | category | flops | bytes accessed | tf_op | source)
XLA Modules:
  0.0 201.3 jit_solution(14253598573891175818)
XLA Ops:
  6.5 0.0 all-gather.3.cloned.1.call-start
  6.5 0.7 all-gather.3.cloned.1.call-update
  7.3 0.0 all-gather.5.cloned.1.call-start
  7.3 50.0 %all-gather.3.cloned.1.call-done = f32[256,2048]{1,0:T(8,128)} async-done(((f32[256,512]{1,0:T(8,128)}), f32[256,2048]{1,0:T(8,128)}) %all-gather.3.cloned.1.call-update) | async-done | bytes 2097168 | tf_op jit(solution)/shard_map/all_gather | solution.py:9
  57.3 0.0 all-gather.5.cloned.1.call-update
  57.3 90.4 %all-gather.5.cloned.1.call-done = f32[2048,2048]{1,0:T(8,128)} async-done(((f32[256,2048]{1,0:T(8,128)}), f32[2048,2048]{1,0:T(8,128)}) %all-gather.5.cloned.1.call-update) | async-done | bytes 16777232 | tf_op jit(solution)/shard_map/all_gather | solution.py:12
  147.8 46.7 %fusion.2 = f32[2,384,2048]{2,1,0:T(8,128)} fusion(f32[2,384,2048]{2,1,0:T(8,128)} %param.4, f32[2,384,2048]{2,1,0:T(8,128)} %param.3, f32[2048,2048]{1,0:T(8,128)} %all-gather.5.cloned.1.call-done), kind=kOutput, calls=%fused_computation.2 | convolution fusion | flops 38656278528 | bytes 35651584 | tf_op jit(solution)/shard_map/dot_general | solution.py:10
Async XLA Ops:
  6.5 50.8 %all-gather.3.cloned.1.call-start = ((), (), s32[]{:S(2)}) async-start(), calls=%async_computation | async-start | bytes 2621440 | tf_op jit(solution)/shard_map/all_gather | solution.py:9
  7.3 140.5 %all-gather.5.cloned.1.call-start = ((), (), s32[]{:S(2)}) async-start(), calls=%async_computation.1 | async-start | bytes 18874368 | tf_op jit(solution)/shard_map/all_gather | solution.py:12
Sparse Core Ops, SparseCore 0:
  8.9 48.3 all-gather.2
  59.2 88.5 all-gather.4
where the time goes:
time: 201 us
  waiting for transfers between devices  141 us (70%)
  matrix products  46.7 us (23%)
  between operations  13.4 us (7%)
    all_gather x1, waiting for transfers between devices, body(): lax.all_gather(panel, 'row', axis=0, tiled=True)  90.4 us
    all_gather x1, waiting for transfers between devices, body(): panel = lax.all_gather(multipliers, 'col', axis=1, tiled=True)  50 us
    dot_general x1, matrix products, body(): jnp.dot(stacked, lax.all_gather(panel, 'row', axis=0, tiled=True), precis...  46.7 us
  transfers between devices with their start and end apart: 2, of which 2 were waited for; matrix products, arithmetic and copies ran while one was open for 0% of the time, Pallas kernels for 0%

commit v1 on v0

v1 whole, which is shorter than its diff:
```python
import functools

import jax
import jax.numpy as jnp
from jax import lax
from jax.experimental import pallas as pl
from jax.experimental.pallas import tpu as pltpu
from jax.sharding import PartitionSpec as P

MESH = pl.DeviceIdType.MESH
CORES, XS = 2, 2
ORDERS = ("zxy", "zyx", "xzy", "yzx")


def pieces_of(depth):
    small = depth * 3 // 16
    large = depth // 2 - small
    cuts, start = [], 0
    for rows in (small, small, large, large):
        cuts.append((start, rows))
        start += rows
    return cuts


def kernel(rows, cols, coeffs, forces, block, out, lam, staged, high, low, total, lam_high, lam_low,
           local_sem, out_sem, near_send, z_send, pair_send, recv, pair_recv):
    ys = rows // (CORES * XS)
    depth, width = block.shape
    half = coeffs.shape[1]
    pieces = pieces_of(depth)
    row, z = lax.axis_index("row"), lax.axis_index("col")
    core, x, y = lax.rem(row, CORES), lax.rem(row // CORES, XS), row // (CORES * XS)

    def row_at(dy, dx, of_core=core):
        return (lax.rem(y + dy, ys) * XS + lax.rem(x + dx, XS)) * CORES + of_core

    def base(r, c):
        return (c * rows + r) * depth

    own = pltpu.make_async_copy(block, lam.at[pl.ds(pl.multiple_of(base(row, z), 8), depth)], local_sem.at[0])
    own.start()
    loads = []
    for part in range(2):
        load = pltpu.make_async_copy(coeffs.at[part], staged.at[pl.ds(part * half, half)], local_sem.at[1 + part])
        load.start()
        loads.append(load)
    for part in range(2):
        for c in range(cols):
            load = pltpu.make_async_copy(
                forces.at[part, :, pl.ds(c * width, width)],
                total.at[c, pl.ds(part * half, half)],
                local_sem.at[3 + part * cols + c],
            )
            load.start()
            loads.append(load)

    near = [(0, 1)] + [(dy, 0) for dy in range(1, ys)]
    targets = [row_at(dy, dx) for dy, dx in near]
    partner = row + 1 - 2 * core
    barrier = pltpu.get_barrier_semaphore()
    for target in targets + [partner]:
        pl.semaphore_signal(barrier, inc=1, device_id={"row": target, "col": z}, device_id_type=MESH)

    @pl.when(z > 0)
    def _():
        pl.semaphore_signal(barrier, inc=1, device_id={"row": row, "col": z - 1}, device_id_type=MESH)

    @pl.when(z < cols - 1)
    def _():
        pl.semaphore_signal(barrier, inc=1, device_id={"row": row, "col": z + 1}, device_id_type=MESH)

    along = jnp.where(z > 0, 1, 0) + jnp.where(z < cols - 1, 1, 0)
    pl.semaphore_wait(barrier, len(near) + 1 + along)
    own.wait()

    def piece_copy(kind, r, c, send_sem, to_row, to_col):
        start, count = pieces[kind]
        place = lam.at[pl.ds(pl.multiple_of(base(r, c) + start, 8), count)]
        return pltpu.make_async_remote_copy(
            src_ref=place, dst_ref=place, send_sem=send_sem, recv_sem=recv.at[kind, r // CORES, c],
            device_id={"row": to_row, "col": to_col}, device_id_type=MESH,
        )

    sent = [0] * len(near)

    def take(kind, dy, dx, c, first):
        r = row_at(dy, dx)
        if not (first and dy == 0 and dx == 0):
            piece_copy(kind, r, c, near_send.at[0], row, z).wait_recv()
        order = ORDERS[kind]
        came = {"x": dx != 0, "y": dy != 0, "z": not first}
        last = max([order.index(axis) for axis in "xyz" if came[axis]], default=-1)
        if order.index("z") > last:
            @pl.when(z > 0)
            def _():
                piece_copy(kind, r, c, z_send.at[0, c], row, z - 1).start()

            @pl.when(z < cols - 1)
            def _():
                piece_copy(kind, r, c, z_send.at[1, c], row, z + 1).start()
        elif order.index("z") == last:
            @pl.when((c > z) & (z > 0))
            def _():
                piece_copy(kind, r, c, z_send.at[0, c], row, z - 1).start()

            @pl.when((c < z) & (z < cols - 1))
            def _():
                piece_copy(kind, r, c, z_send.at[1, c], row, z + 1).start()
        for way, (sy, sx) in enumerate(near):
            if order.index("x" if sx else "y") > last:
                piece_copy(kind, r, c, near_send.at[way], targets[way], z).start()

    def spread(c, first):
        for kind in range(4):
            take(kind, 0, 0, c, first)
        if first:
            take(2, 0, 1, c, first)
            for dy in range(1, ys):
                take(3, dy, 0, c, first)
        take(0, 0, 1, c, first)
        for dy in range(1, ys):
            take(1, dy, 0, c, first)
        if not first:
            take(2, 0, 1, c, first)
            for dy in range(1, ys):
                take(3, dy, 0, c, first)

    def pair_copy(r, c):
        place = lam.at[pl.ds(pl.multiple_of(base(r, c), 8), depth)]
        return pltpu.make_async_remote_copy(
            src_ref=place, dst_ref=place, send_sem=pair_send, recv_sem=pair_recv.at[r // CORES, c],
            device_id={"row": partner, "col": z}, device_id_type=MESH,
        )

    def multiply(r, c):
        held = lam[pl.ds(pl.multiple_of(base(r, c), 8), depth), :]
        rounded = held.astype(jnp.bfloat16)
        lam_high[...] = rounded
        lam_low[...] = (held - rounded.astype(jnp.float32)).astype(jnp.bfloat16)

        @pl.loop(0, 2)
        def _(part):
            here = pl.ds(pl.multiple_of(part * half, 8), half)
            a_high, a_low = high[r, here, :], low[r, here, :]
            product = jnp.dot(a_high, lam_high[...], preferred_element_type=jnp.float32)
            product += jnp.dot(a_high, lam_low[...], preferred_element_type=jnp.float32)
            product += jnp.dot(a_low, lam_high[...], preferred_element_type=jnp.float32)
            total[c, here, :] -= product

    def store(c):
        return [
            pltpu.make_async_copy(
                total.at[c, pl.ds(part * half, half)],
                out.at[part, :, pl.ds(pl.multiple_of(c * width, 128), width)],
                out_sem.at[part, c],
            )
            for part in range(2)
        ]

    def finish(c, first):
        pair_copy(row, c).start()
        for kind in (1, 3):
            take(kind, 0, 1, c, first)
        pair_copy(row_at(0, 1), c).start()
        for dy in range(1, ys):
            for kind in (0, 2):
                take(kind, dy, 0, c, first)
            pair_copy(row_at(dy, 0), c).start()
        for dy in range(1, ys):
            for kind in range(4):
                take(kind, dy, 1, c, first)
            pair_copy(row_at(dy, 1), c).start()

        @pl.loop(0, rows // CORES)
        def _(q):
            multiply(q * CORES + core, c)

        @pl.loop(0, rows // CORES)
        def _(q):
            r = q * CORES + 1 - core
            pair_copy(r, c).wait_recv()
            multiply(r, c)

        for copy in store(c):
            copy.start()

    def column(j):
        edge = jnp.minimum(z, cols - 1 - z)
        longer = jnp.where(z < cols // 2, 1, -1)
        near_by = longer * (1 - 2 * lax.rem(j + 1, 2)) * ((j + 1) // 2)
        return z + jnp.where(j <= 2 * edge, near_by, longer * (j - edge))

    spread(z, True)
    for load in loads:
        load.wait()
    for r in range(rows):
        value = staged[:, r * depth:(r + 1) * depth]
        rounded = value.astype(jnp.bfloat16)
        high[r] = rounded
        low[r] = (value - rounded.astype(jnp.float32)).astype(jnp.bfloat16)

    spread(column(1), False)
    finish(z, True)

    @pl.loop(2, cols)
    def _(j):
        spread(column(j), False)
        finish(column(j - 1), False)

    finish(column(cols - 1), False)

    def drain(count, sem):
        span = lam.at[pl.ds(0, count)]
        pltpu.make_async_remote_copy(
            src_ref=span, dst_ref=span, send_sem=sem, recv_sem=recv.at[0, 0, 0],
            device_id={"row": partner, "col": z}, device_id_type=MESH,
        ).wait_send()

    small, large = pieces[0][1], pieces[2][1]
    for way, (sy, sx) in enumerate(near):
        if sx:
            count = cols * small + cols * ys * small + large + cols * ys * large
        else:
            count = cols * XS * small + cols * small + cols * XS * large + large
        drain(count, near_send.at[way])
    drain(cols * (rows // CORES) * depth, pair_send)
    along_z = 2 * small + XS * large + ys * large

    @pl.loop(0, cols)
    def _(c):
        @pl.when((c >= z) & (z > 0))
        def _():
            drain(along_z, z_send.at[0, c])

        @pl.when((c <= z) & (z < cols - 1))
        def _():
            drain(along_z, z_send.at[1, c])

        for copy in store(c):
            copy.wait()


def body(rows, cols, coeffs, forces, multipliers):
    parts, half, orbitals = coeffs.shape
    depth, width = multipliers.shape
    count = parts * half
    near = rows // (CORES * XS)
    return pl.pallas_call(
        functools.partial(kernel, rows, cols),
        out_shape=jax.ShapeDtypeStruct(coeffs.shape, jnp.float32),
        in_specs=[pl.BlockSpec(memory_space=pl.ANY)] * 3,
        out_specs=pl.BlockSpec(memory_space=pl.ANY),
        scratch_shapes=[
            pltpu.VMEM((rows * cols * depth, width), jnp.float32),
            pltpu.VMEM((count, orbitals), jnp.float32),
            pltpu.VMEM((rows, count, depth), jnp.bfloat16),
            pltpu.VMEM((rows, count, depth), jnp.bfloat16),
            pltpu.VMEM((cols, count, width), jnp.float32),
            pltpu.VMEM((depth, width), jnp.bfloat16),
            pltpu.VMEM((depth, width), jnp.bfloat16),
            pltpu.SemaphoreType.DMA((3 + 2 * cols,)),
            pltpu.SemaphoreType.DMA((2, cols)),
            pltpu.SemaphoreType.DMA((near,)),
            pltpu.SemaphoreType.DMA((2, cols)),
            pltpu.SemaphoreType.DMA,
            pltpu.SemaphoreType.DMA((4, rows // CORES, cols)),
            pltpu.SemaphoreType.DMA((rows // CORES, cols)),
        ],
        compiler_params=pltpu.CompilerParams(
            collective_id=0, has_side_effects=True, vmem_limit_bytes=60 * 1024 * 1024
        ),
    )(coeffs, forces, multipliers)


def solution(mesh):
    placed = (P(None, ("row", "col"), None), P(None, ("row", "col"), None), P("row", "col"))
    rows, cols = mesh.shape["row"], mesh.shape["col"]
    return jax.shard_map(
        functools.partial(body, rows, cols), mesh=mesh, in_specs=placed,
        out_specs=P(None, ("row", "col"), None), check_vma=False,
    )
```

time: 201 us -> 94.9 us (0.47)
  waiting for transfers between devices: 141 us -> 0 us
  Pallas kernels: 0 us -> 88.4 us
  matrix products: 46.7 us -> 0 us
  between operations: 13.4 us -> 0.01 us
  local copies, waits for them, and re-layouts: 0 us -> 6.29 us
    all_gather x2 -> x0, waiting for transfers between devices: 140 us -> none  [the longest x1 90.4 us: body(): lax.all_gather(panel, 'row', axis=0, tiled=True)]
    pallas_call x0 -> x1, Pallas kernels: none -> 88.4 us  [body(): pl.pallas_call(functools.partial(kernel, rows, cols), out_shape=jax.Shape...]
    dot_general x1 -> x0, matrix products: 46.7 us -> none  [body(): jnp.dot(stacked, lax.all_gather(panel, 'row', axis=0, tiled=True), precis...]
    unnamed x0 -> x1, local copies, waits for them, and re-layouts: none -> 6.29 us
  transfers between devices with their start and end apart: 2 -> 0, of which waited for: 2 -> 0; matrix products, arithmetic and copies ran while one was open for 0% -> 0% of each run, Pallas kernels for 0% -> 0%
where the time goes in v1:
time: 94.9 us; the launch traced here: 94.7 us
  Pallas kernels  88.4 us (93%)
  local copies, waits for them, and re-layouts  6.29 us (7%)
    pallas_call x1, Pallas kernels, body(): pl.pallas_call(functools.partial(kernel, rows, cols), out_shape=jax.Shape...  88.4 us
    unnamed x1, local copies, waits for them, and re-layouts  6.29 us

profile of v1, /device:TPU:0, one launch (start us, length us, event | category | flops | bytes accessed | tf_op | source)
XLA Modules:
  0.0 94.7 jit_solution(14465788679063661392)
XLA Ops:
  0.0 88.4 %shard_map.37 = f32[2,384,2048]{2,1,0:T(8,128)} custom-call(f32[2,384,2048]{2,1,0:T(8,128)} %coeffs.1, f32[2,384,2048]{2,1,0:T(8,128)} %forces.1, f32[256,512]{1,0:T(8,128)} %block.1), custom_call_target="tpu_custom_call" | custom-call | tf_op jit(solution)/shard_map/pallas_call | solution.py:248
  88.4 6.3 %copy.5 = f32[2,384,2048]{2,1,0:T(8,128)} copy(f32[2,384,2048]{2,1,0:T(8,128)} %shard_map.37) | data formatting | bytes 12582912

commit v2 on v1

--- a/solution.py
+++ b/solution.py
@@ -22,8 +22,8 @@
     return cuts
 
 
-def kernel(rows, cols, coeffs, forces, block, out, lam, staged, high, low, total, lam_high, lam_low,
-           local_sem, out_sem, near_send, z_send, pair_send, recv, pair_recv):
+def kernel(rows, cols, coeffs, forces, block, out, lam, staged, high, low, lam_high, lam_low,
+           local_sem, near_send, z_send, pair_send, recv, pair_recv):
     ys = rows // (CORES * XS)
     depth, width = block.shape
     half = coeffs.shape[1]
@@ -45,14 +45,9 @@
         load.start()
         loads.append(load)
     for part in range(2):
-        for c in range(cols):
-            load = pltpu.make_async_copy(
-                forces.at[part, :, pl.ds(c * width, width)],
-                total.at[c, pl.ds(part * half, half)],
-                local_sem.at[3 + part * cols + c],
-            )
-            load.start()
-            loads.append(load)
+        load = pltpu.make_async_copy(forces.at[part], out.at[part], local_sem.at[3 + part])
+        load.start()
+        loads.append(load)
 
     near = [(0, 1)] + [(dy, 0) for dy in range(1, ys)]
     targets = [row_at(dy, dx) for dy, dx in near]
@@ -110,9 +105,13 @@
             if order.index("x" if sx else "y") > last:
                 piece_copy(kind, r, c, near_send.at[way], targets[way], z).start()
 
-    def spread(c, first):
-        for kind in range(4):
+    def spread(c, first, fill):
+        for kind in (0, 1):
             take(kind, 0, 0, c, first)
+        fill(0)
+        for kind in (2, 3):
+            take(kind, 0, 0, c, first)
+            fill(kind - 1)
         if first:
             take(2, 0, 1, c, first)
             for dy in range(1, ys):
@@ -120,8 +119,10 @@
         take(0, 0, 1, c, first)
         for dy in range(1, ys):
             take(1, dy, 0, c, first)
+        fill(3)
         if not first:
             take(2, 0, 1, c, first)
+            fill(4)
             for dy in range(1, ys):
                 take(3, dy, 0, c, first)
 
@@ -145,44 +146,53 @@
             product = jnp.dot(a_high, lam_high[...], preferred_element_type=jnp.float32)
             product += jnp.dot(a_high, lam_low[...], preferred_element_type=jnp.float32)
             product += jnp.dot(a_low, lam_high[...], preferred_element_type=jnp.float32)
-            total[c, here, :] -= product
-
-    def store(c):
-        return [
-            pltpu.make_async_copy(
-                total.at[c, pl.ds(part * half, half)],
-                out.at[part, :, pl.ds(pl.multiple_of(c * width, 128), width)],
-                out_sem.at[part, c],
-            )
-            for part in range(2)
-        ]
-
-    def finish(c, first):
+            out[part, :, pl.ds(pl.multiple_of(c * width, 128), width)] -= product
+
+    def settle(c, first, own, other):
         pair_copy(row, c).start()
+        own(0, 0)
         for kind in (1, 3):
             take(kind, 0, 1, c, first)
         pair_copy(row_at(0, 1), c).start()
+        own(0, 1)
+        other(0, 0)
         for dy in range(1, ys):
             for kind in (0, 2):
                 take(kind, dy, 0, c, first)
             pair_copy(row_at(dy, 0), c).start()
+            own(dy, 0)
+        other(0, 1)
         for dy in range(1, ys):
             for kind in range(4):
                 take(kind, dy, 1, c, first)
             pair_copy(row_at(dy, 1), c).start()
-
-        @pl.loop(0, rows // CORES)
-        def _(q):
-            multiply(q * CORES + core, c)
-
-        @pl.loop(0, rows // CORES)
-        def _(q):
-            r = q * CORES + 1 - core
+            own(dy, 1)
+        for dy in range(1, ys):
+            other(dy, 0)
+            other(dy, 1)
+
+    def own_block(c):
+        return lambda dy, dx: multiply(row_at(dy, dx), c)
+
+    def other_block(c):
+        def run(dy, dx):
+            r = row_at(dy, dx, 1 - core)
             pair_copy(r, c).wait_recv()
             multiply(r, c)
-
-        for copy in store(c):
-            copy.start()
+        return run
+
+    def fill_with(c, first):
+        places = [(dy, dx) for dy in range(ys) for dx in range(XS)]
+        work = [(own_block(c), place) for place in places] + [(other_block(c), place) for place in places]
+
+        def fill(turn):
+            if turn == 0:
+                settle(c, first, lambda *_: None, lambda *_: None)
+            else:
+                share = len(work) // 4
+                for run, place in work[(turn - 1) * share:turn * share]:
+                    run(*place)
+        return fill
 
     def column(j):
         edge = jnp.minimum(z, cols - 1 - z)
@@ -190,7 +200,7 @@
         near_by = longer * (1 - 2 * lax.rem(j + 1, 2)) * ((j + 1) // 2)
         return z + jnp.where(j <= 2 * edge, near_by, longer * (j - edge))
 
-    spread(z, True)
+    spread(z, True, lambda turn: None)
     for load in loads:
         load.wait()
     for r in range(rows):
@@ -199,15 +209,18 @@
         high[r] = rounded
         low[r] = (value - rounded.astype(jnp.float32)).astype(jnp.bfloat16)
 
-    spread(column(1), False)
-    finish(z, True)
+    def step(j, first):
+        c = column(j - 1)
+        spread(column(j), False, fill_with(c, first))
+
+    step(1, True)
 
     @pl.loop(2, cols)
     def _(j):
-        spread(column(j), False)
-        finish(column(j - 1), False)
-
-    finish(column(cols - 1), False)
+        step(j, False)
+
+    last = column(cols - 1)
+    settle(last, False, own_block(last), other_block(last))
 
     def drain(count, sem):
         span = lam.at[pl.ds(0, count)]
@@ -236,9 +249,6 @@
         def _():
             drain(along_z, z_send.at[1, c])
 
-        for copy in store(c):
-            copy.wait()
-
 
 def body(rows, cols, coeffs, forces, multipliers):
     parts, half, orbitals = coeffs.shape
@@ -247,19 +257,17 @@
     near = rows // (CORES * XS)
     return pl.pallas_call(
         functools.partial(kernel, rows, cols),
-        out_shape=jax.ShapeDtypeStruct(coeffs.shape, jnp.float32),
-        in_specs=[pl.BlockSpec(memory_space=pl.ANY)] * 3,
-        out_specs=pl.BlockSpec(memory_space=pl.ANY),
+        out_shape=pltpu.VMEM(coeffs.shape, jnp.float32),
+        in_specs=[pl.BlockSpec(memory_space=pltpu.HBM)] * 3,
+        out_specs=pl.BlockSpec(memory_space=pltpu.VMEM),
         scratch_shapes=[
             pltpu.VMEM((rows * cols * depth, width), jnp.float32),
             pltpu.VMEM((count, orbitals), jnp.float32),
             pltpu.VMEM((rows, count, depth), jnp.bfloat16),
             pltpu.VMEM((rows, count, depth), jnp.bfloat16),
-            pltpu.VMEM((cols, count, width), jnp.float32),
             pltpu.VMEM((depth, width), jnp.bfloat16),
             pltpu.VMEM((depth, width), jnp.bfloat16),
-            pltpu.SemaphoreType.DMA((3 + 2 * cols,)),
-            pltpu.SemaphoreType.DMA((2, cols)),
+            pltpu.SemaphoreType.DMA((5,)),
             pltpu.SemaphoreType.DMA((near,)),
             pltpu.SemaphoreType.DMA((2, cols)),
             pltpu.SemaphoreType.DMA,
@@ -267,7 +275,7 @@
             pltpu.SemaphoreType.DMA((rows // CORES, cols)),
         ],
         compiler_params=pltpu.CompilerParams(
-            collective_id=0, has_side_effects=True, vmem_limit_bytes=60 * 1024 * 1024
+            collective_id=0, has_side_effects=True, vmem_limit_bytes=48 * 1024 * 1024
         ),
     )(coeffs, forces, multipliers)
 

time: 94.9 us -> 79.9 us (0.84)
  Pallas kernels: 88.4 us -> 77.1 us
  local copies, waits for them, and re-layouts: 6.29 us -> 2.71 us
    pallas_call x1, Pallas kernels: 88.4 us -> 77.1 us  [body(): pl.pallas_call(functools.partial(kernel, rows, cols), out_shape=pltpu.VME...]
    unnamed x1, local copies, waits for them, and re-layouts: 6.29 us -> 2.71 us
where the time goes in v2:
time: 79.9 us; the launch traced here: 79.8 us
  Pallas kernels  77.1 us (96%)
  local copies, waits for them, and re-layouts  2.71 us (3%)
    pallas_call x1, Pallas kernels, body(): pl.pallas_call(functools.partial(kernel, rows, cols), out_shape=pltpu.VME...  77.1 us
    unnamed x1, local copies, waits for them, and re-layouts  2.71 us

profile of v2, /device:TPU:0, one launch (start us, length us, event | category | flops | bytes accessed | tf_op | source)
XLA Modules:
  0.0 79.8 jit_solution(2783580328817454350)
XLA Ops:
  0.0 77.1 %shard_map.37 = f32[2,384,2048]{2,1,0:T(8,128)S(1)} custom-call(f32[2,384,2048]{2,1,0:T(8,128)} %coeffs.1, f32[2,384,2048]{2,1,0:T(8,128)} %forces.1, f32[256,512]{1,0:T(8,128)} %block.1), custom_call_target="tpu_custom_call" | custom-call | tf_op jit(solution)/shard_map/pallas_call | solution.py:258
  77.1 2.7 %copy.5 = f32[2,384,2048]{2,1,0:T(8,128)} copy(f32[2,384,2048]{2,1,0:T(8,128)S(1)} %shard_map.37) | data formatting | bytes 12582912
